TPU v7x, 32 devices: a whole 2x2x4 slice. The times are simulated.
32 devices in a mesh: kgrp: 2 (over y), pw: 4 (over z), band: 4 (over x, core).
Axes of the slice: x: 2, y: 2, z: 4, core: 2. Of those that a mesh axis runs over, the one named last changes fastest.
Arguments:
- waves: float32 [128, 4, 16, 256], P('band', 'kgrp', 'pw'), parts along dimension 1, as said below
- forward: float32 [128, 4, 16, 256], P('band', 'kgrp', 'pw'), parts along dimension 1, as said below
- backward: float32 [128, 4, 16, 256], P('band', 'kgrp', 'pw'), parts along dimension 1, as said below
- projectors: float32 [256, 2, 16, 256], P('kgrp', None, 'pw'), parts along dimension 0, as said below
- potential: float32 [256, 16], P('pw'), may hold values from 0.25 to 2
- strengths: float32 [128], replicated, may hold values from 0.5 to 4
- shifts: float32 [128], P('band'), may hold values from 0.5 to 2
Outputs:
- response: float32 [128, 4, 16, 256], P('band', 'kgrp', 'pw'), parts along dimension 1
- derivative: float32 [128, 4, 16, 256], P('band', 'kgrp', 'pw'), parts along dimension 1
There are 2 independent parts, one for each index of `kgrp`. A program takes and returns all parts, laid end to end along the dimension named above; an argument that names none is the same for every part. Nothing has to cross between parts.
Inputs may be any that keep to these rules, and one draw needn't show every extreme that they name: `waves`: real and imaginary parts of every band's coefficients are drawn independently at every grid point. `forward`: the margin of the slab's bands with these coefficients is an invertible matrix. `backward`: the margin of the slab's bands with these coefficients is an invertible matrix. `projectors`: real and imaginary parts of every projector are drawn independently at every grid point.
All inputs are finite; a program needn't handle non-finite values.
Results may differ from a plain program's by a relative error of at most 0.0003.
Values sent between devices are 32-bit elements; how exact they have to be, the bound alone decides.
A program may use at most 64 MiB of HBM per device.

v0:
```python
import math

import jax
import jax.numpy as jnp
from jax import lax
from jax.sharding import PartitionSpec as P

ITERS = 2


precise = lax.Precision.HIGHEST
string_step = 0.05
kinetic_scale = 4.0


def margin(left_set, right_set):
    products = jnp.einsum("ixg,jyg->xyij", left_set, right_set, precision=precise)
    return jnp.stack([products[0, 0] + products[1, 1], products[0, 1] - products[1, 0]])


def combine(vectors, coeffs):
    table = jnp.stack([jnp.stack([coeffs[0], coeffs[1]]), jnp.stack([-coeffs[1], coeffs[0]])])
    return jnp.einsum("ixg,xyij->jyg", vectors, table, precision=precise)


def invert(matrix):
    real_part = matrix[0]
    imag_part = matrix[1]
    embedded = jnp.concatenate(
        [jnp.concatenate([real_part, -imag_part], 1), jnp.concatenate([imag_part, real_part], 1)], 0
    )
    normal = jnp.dot(embedded.T, embedded, precision=precise)
    lower_factor = jnp.linalg.cholesky(normal)
    middle = lax.linalg.triangular_solve(lower_factor, embedded.T, left_side=True, lower=True)
    inverse = lax.linalg.triangular_solve(
        lower_factor, middle, left_side=True, lower=True, transpose_a=True
    )
    count_rows = real_part.shape[0]
    return jnp.stack([inverse[:count_rows, :count_rows], inverse[count_rows:, :count_rows]])


def centred(index, length):
    shifted = (index + length // 2) % length - length // 2
    return shifted.astype(jnp.float32) / length


def dft_table(length, sign):
    index = jnp.arange(length, dtype=jnp.int32)
    phase = index[:, None] * index[None, :] % length
    angle = phase.astype(jnp.float32) * (2.0 * math.pi / length)
    cosine = jnp.cos(angle) / math.sqrt(length)
    sine = sign * jnp.sin(angle) / math.sqrt(length)
    return jnp.stack([jnp.stack([cosine, sine]), jnp.stack([-sine, cosine])])


def body(waves, forward, backward, projectors, potential, strengths, shifts):
    bands = waves.shape[0]
    rows = waves.shape[2]
    width = waves.shape[3]
    peers = lax.axis_size("pw")
    length = rows * peers
    points = float(length * width)
    cells = rows * width
    quarter = width // peers
    waves_flat = waves.reshape(bands, 2, cells)
    forward_flat = forward.reshape(bands, 2, cells)
    backward_flat = backward.reshape(bands, 2, cells)
    offset = lax.axis_index("band") * bands
    every_wave = lax.all_gather(waves_flat, "band", axis=0, tiled=True)
    forward_part = margin(every_wave, forward_flat) / points
    backward_part = margin(every_wave, backward_flat) / points
    forward_part, backward_part = lax.psum((forward_part, backward_part), "pw")
    forward_whole, backward_whole = (
        lax.all_gather(forward_part, "band", axis=2, tiled=True),
        lax.all_gather(backward_part, "band", axis=2, tiled=True),
    )
    forward_inverse = invert(forward_whole)
    backward_inverse = -invert(backward_whole)
    forward_cols = lax.dynamic_slice_in_dim(forward_inverse, offset, bands, 2)
    backward_cols = lax.dynamic_slice_in_dim(backward_inverse, offset, bands, 2)
    moved = combine(
        lax.all_gather(forward_flat, "band", axis=0, tiled=True), forward_cols
    ) + combine(lax.all_gather(backward_flat, "band", axis=0, tiled=True), backward_cols)
    derivative = (moved / (2.0 * string_step)).reshape(bands, 2, rows, width)
    first_index = lax.axis_index("pw") * rows + jnp.arange(rows, dtype=jnp.int32)
    second_index = jnp.arange(width, dtype=jnp.int32)
    first_freq = centred(first_index, length)
    second_freq = centred(second_index, width)
    kinetic = kinetic_scale * (
        first_freq[:, None] * first_freq[:, None] + second_freq[None, :] * second_freq[None, :]
    )
    diagonal = kinetic[None, None] + shifts[:, None, None, None]
    width_out = dft_table(width, 1.0)
    width_back = dft_table(width, -1.0)
    long_out = dft_table(length, 1.0).reshape(2, 2, peers, rows, length)
    long_back = dft_table(length, -1.0).reshape(2, 2, length, peers, rows)
    projector_flat = projectors.reshape(projectors.shape[0], 2, cells)
    residual = -derivative
    direction = residual
    solution = jnp.zeros_like(residual)
    norm_now = lax.psum(jnp.sum(residual * residual, axis=(1, 2, 3)), "pw")
    for turn in range(ITERS):
        sectioned = jnp.einsum("bxrj,xyjk->ykrb", direction, width_out, precision=precise).reshape(
            2, width, rows * bands
        )
        arrived = lax.all_to_all(sectioned, "pw", split_axis=1, concat_axis=2, tiled=True).reshape(
            2, quarter, peers, rows, bands
        )
        field = jnp.einsum("xqsrb,xysrk->yqbk", arrived, long_out, precision=precise)
        weighted = field * potential[None, :, None, :]
        leaving = jnp.einsum("xqbk,xyksr->yqsrb", weighted, long_back, precision=precise).reshape(
            2, quarter, peers * rows * bands
        )
        returned = lax.all_to_all(leaving, "pw", split_axis=2, concat_axis=1, tiled=True).reshape(
            2, width, rows, bands
        )
        smooth_part = jnp.einsum("xkrb,xykj->byrj", returned, width_back, precision=precise)
        coupling = margin(projector_flat, direction.reshape(bands, 2, cells)) / points
        own_energy = jnp.sum(diagonal * direction * direction, axis=(1, 2, 3)) + jnp.sum(
            weighted * field, axis=(0, 1, 3)
        )
        coupling, own_energy = lax.psum((coupling, own_energy), "pw")
        nonlocal_part = combine(projector_flat, coupling * strengths[None, :, None]).reshape(
            direction.shape
        )
        image = diagonal * direction + smooth_part + nonlocal_part
        curvature = own_energy + points * jnp.sum(
            strengths[None, :, None] * coupling * coupling, axis=(0, 1)
        )
        image, curvature = (image, curvature)
        alpha = (norm_now / curvature)[:, None, None, None]
        solution = solution + alpha * direction
        if turn + 1 < ITERS:
            residual = residual - alpha * image
            norm_next = lax.psum(jnp.sum(residual * residual, axis=(1, 2, 3)), "pw")
            direction = residual + (norm_next / norm_now)[:, None, None, None] * direction
            norm_now = norm_next
    return (solution, derivative)


def solution(mesh):
    in_specs = (
        P("band", "kgrp", "pw", None),
        P("band", "kgrp", "pw", None),
        P("band", "kgrp", "pw", None),
        P("kgrp", None, "pw", None),
        P("pw", None),
        P(),
        P("band"),
    )
    out_specs = (P("band", "kgrp", "pw", None), P("band", "kgrp", "pw", None))
    return jax.shard_map(body, mesh=mesh, in_specs=in_specs, out_specs=out_specs, check_vma=False)
```

profile of v0, /device:TPU:0, one launch (start us, length us, event | category | flops | bytes accessed | tf_op | source)
XLA Modules:
  0.0 366.6 jit_solution(16104414483020477694)
XLA Ops:
  10.6 19.0 %all-gather.4.cloned.1.call-done = f32[128,2,1024]{2,0,1:T(8,128)} async-done(((f32[32,2,1024]{2,0,1:T(8,128)}), f32[128,2,1024]{2,0,1:T(8,128)}) %all-gather.4.cloned.1.call-update) | async-done | bytes 1048592 | tf_op jit(solution)/shard_map/all_gather | solution.py:69
  29.6 2.4 convolution_bitcast_fusion.11
  45.4 2.4 fusion.20
  47.8 20.5 %all-reduce.6.cloned.1.call-done = (f32[2,128,32]{1,2,0:T(8,128)}, f32[2,128,32]{1,2,0:T(8,128)}) async-done(((f32[2,128,32]{1,2,0:T(8,128)}, f32[2,128,32]{1,2,0:T(8,128)}), (f32[2,128,32]{1,2,0:T(8,128)}, f32[2,128,32]{1,2,0:T(8,128)})) %all-reduce.6.cloned.1.call-update) | async-done | bytes 65552 | tf_op jit(solution)/shard_map/psum | solution.py:72
  68.3 5.8 %all_gather.16 = f32[2,128,128]{1,2,0:T(8,128)S(1)} all-gather(f32[2,128,32]{1,2,0:T(8,128)} %get-tuple-element.71), channel_id=1, replica_groups=mesh['kgrp'=2,'pw'=4,'band'=4] {'band'}, dimensions={2}, use_global_device_ids=true | all-gather | bytes 163840 | tf_op jit(solution)/shard_map/all_gather | solution.py:74
  77.8 11.7 %cholesky.130 = f32[128,128]{1,0:T(8,128)S(1)} custom-call(f32[128,128]{1,0:T(8,128)S(1)} %cholesky.194), custom_call_target="Cholesky" | custom-call | tf_op jit(solution)/shard_map/jit(cholesky)/cholesky | solution.py:33
  90.2 10.4 %custom-call.17 = f32[1,128,128]{1,2,0:T(8,128)} custom-call(f32[1,128,128]{2,1,0:T(8,128)S(1)} %get-tuple-element.93), custom_call_target="InvertDiagBlocksLowerTriangular" | custom-call | tf_op jit(solution)/shard_map/jit(cholesky)/cholesky | solution.py:33
  102.7 13.2 %cholesky.147 = f32[128,128]{1,0:T(8,128)} custom-call(f32[128,128]{1,0:T(8,128)} %convolution_subtract_fusion.3), custom_call_target="Cholesky" | custom-call | tf_op jit(solution)/shard_map/jit(cholesky)/cholesky | solution.py:33
  122.5 6.6 %while.8 = (s32[]{:T(128)}, f32[256,256]{1,0:T(8,128)S(1)}, s32[2,2]{1,0:T(2,128)}, f32[2,128,128]{2,1,0:T(8,128)}, s32[]{:T(128)}) while((s32[]{:T(128)}, f32[256,256]{1,0:T(8,128)S(1)}, s32[2,2]{1,0:T(2,128)}, f32[2,128,128]{2,1,0:T(8,128)}, s32[]{:T(128)}) %tuple.88), condition=%wide.while_cond.1, body=%wide.while_body.1.sunk | while | flops 2 | bytes 132797 | solution.py:35
  123.8 2.0 bitcast_dynamic-update-slice_fusion.4
  127.1 2.0 bitcast_dynamic-update-slice_fusion.4
  129.0 21.1 %custom-call.19 = f32[2,128,128]{1,2,0:T(8,128)} custom-call(f32[2,128,128]{2,1,0:T(8,128)} %get-tuple-element.34), custom_call_target="InvertDiagBlocksLowerTriangular" | custom-call | tf_op jit(solution)/shard_map/triangular_solve/custom-call.4 | solution.py:35
  154.0 5.8 %all_gather.18 = f32[2,128,128]{1,2,0:T(8,128)S(1)} all-gather(f32[2,128,32]{1,2,0:T(8,128)S(1)} %copy-done.29), channel_id=1, replica_groups=mesh['kgrp'=2,'pw'=4,'band'=4] {'band'}, dimensions={2}, use_global_device_ids=true | all-gather | bytes 163840 | tf_op jit(solution)/shard_map/all_gather | solution.py:75
  166.0 11.7 %cholesky.164 = f32[128,128]{1,0:T(8,128)S(1)} custom-call(f32[128,128]{1,0:T(8,128)S(1)} %cholesky.197), custom_call_target="Cholesky" | custom-call | tf_op jit(solution)/shard_map/jit(cholesky)/cholesky | solution.py:33
  178.3 10.4 %custom-call.20 = f32[1,128,128]{1,2,0:T(8,128)} custom-call(f32[1,128,128]{2,1,0:T(8,128)S(1)} %get-tuple-element.97), custom_call_target="InvertDiagBlocksLowerTriangular" | custom-call | tf_op jit(solution)/shard_map/jit(cholesky)/cholesky | solution.py:33
  190.9 13.2 %cholesky.181 = f32[128,128]{1,0:T(8,128)} custom-call(f32[128,128]{1,0:T(8,128)} %convolution_subtract_fusion.2), custom_call_target="Cholesky" | custom-call | tf_op jit(solution)/shard_map/jit(cholesky)/cholesky | solution.py:33
  209.8 6.7 %while.9 = (s32[]{:T(128)}, f32[256,256]{1,0:T(8,128)S(1)}, s32[2,2]{1,0:T(2,128)}, f32[2,128,128]{2,1,0:T(8,128)}, s32[]{:T(128)}) while((s32[]{:T(128)}, f32[256,256]{1,0:T(8,128)S(1)}, s32[2,2]{1,0:T(2,128)}, f32[2,128,128]{2,1,0:T(8,128)}, s32[]{:T(128)}) %tuple.100), condition=%wide.while_cond.1.clone, body=%wide.while_body.1.clone.sunk | while | flops 2 | bytes 132797 | solution.py:35
  216.5 21.1 %custom-call.22 = f32[2,128,128]{1,2,0:T(8,128)} custom-call(f32[2,128,128]{2,1,0:T(8,128)} %get-tuple-element.36), custom_call_target="InvertDiagBlocksLowerTriangular" | custom-call | tf_op jit(solution)/shard_map/triangular_solve/custom-call.4 | solution.py:35
  247.3 2.7 convolution_bitcast_fusion.3
  250.0 2.8 fusion.27
  256.0 4.0 %all-to-all-start = ((f32[2,256,128]{2,0,1:T(2,128)}), f32[2,256,128]{2,0,1:T(2,128)}, u32[]{:S(2)}, u32[]{:S(2)}) async-start(f32[2,256,128]{2,0,1:T(2,128)} %copy.164), calls=%async_computation | async-start | bytes 524288 | tf_op jit(solution)/shard_map/all_to_all | solution.py:106
  265.0 4.8 %all-to-all-done = f32[2,256,128]{2,0,1:T(2,128)} async-done(((f32[2,256,128]{2,0,1:T(2,128)}), f32[2,256,128]{2,0,1:T(2,128)}, u32[]{:S(2)}, u32[]{:S(2)}) %all-to-all-start) | async-done | bytes 262176 | tf_op jit(solution)/shard_map/all_to_all | solution.py:106
  273.4 3.3 fusion.22
  279.0 2.3 reshape.679
  281.3 4.0 %all-to-all-start.1 = ((f32[4,1,16384]{2,1,0:T(1,128)}), f32[4,1,16384]{2,1,0:T(1,128)}, u32[]{:S(2)}, u32[]{:S(2)}) async-start(f32[4,1,16384]{2,1,0:T(1,128)} %reshape.679), calls=%async_computation.1 | async-start | bytes 524288 | tf_op jit(solution)/shard_map/all_to_all | solution.py:114
  286.6 21.1 %all-reduce.2 = (f32[2,128,32]{1,2,0:T(8,128)}, f32[32]{0:T(128)S(1)}, f32[32]{0:T(128)S(1)}) all-reduce(f32[2,128,32]{1,2,0:T(8,128)} %maximum_multiply_fusion.2, f32[32]{0:T(128)S(1)} %copy-done.37, f32[32]{0:T(128)S(1)} %add.346), channel_id=1, replica_groups=mesh['kgrp'=2,'pw'=4,'band'=4] {'pw'}, use_global_device_ids=true, to_apply=%region_11.15 | all-reduce | flops 8256 | bytes 66048 | tf_op jit(solution)/shard_map/psum | solution.py:122
  311.5 2.2 reduce.10
  315.6 2.0 multiply_reduce_fusion
  317.7 8.4 %psum.61 = f32[32]{0:T(128)S(1)} all-reduce(f32[32]{0:T(128)S(1)} %get-tuple-element.124), channel_id=1, replica_groups=mesh['kgrp'=2,'pw'=4,'band'=4] {'pw'}, use_global_device_ids=true, to_apply=%region_14.18 | all-reduce | flops 32 | bytes 256 | tf_op jit(solution)/shard_map/psum | solution.py:135
  327.8 3.4 all-to-all-start.2
  332.5 5.8 %all-to-all-done.2 = f32[2,256,128]{2,0,1:T(2,128)S(1)} async-done(((f32[2,256,128]{2,0,1:T(2,128)}), f32[2,256,128]{2,0,1:T(2,128)S(1)}, u32[]{:S(2)}, u32[]{:S(2)}) %all-to-all-start.2) | async-done | bytes 262176 | tf_op jit(solution)/shard_map/all_to_all | solution.py:106
  340.7 18.0 %all-reduce.1 = (f32[32]{0:T(128)S(1)}, f32[2,128,32]{1,2,0:T(8,128)S(1)}) all-reduce(f32[32]{0:T(128)S(1)} %add.357, f32[2,128,32]{1,2,0:T(8,128)S(1)} %maximum_multiply_fusion.3), channel_id=1, replica_groups=mesh['kgrp'=2,'pw'=4,'band'=4] {'pw'}, use_global_device_ids=true, to_apply=%region_17.21 | all-reduce | flops 8224 | bytes 65792 | tf_op jit(solution)/shard_map/psum | solution.py:122
  (235 shorter events, 91.5 us)
Async XLA Ops:
  7.2 22.4 %all-gather.4.cloned.1.call-start = ((), (), s32[]{:S(2)}) async-start(), calls=%async_computation.3 | async-start | bytes 1310720 | tf_op jit(solution)/shard_map/all_gather | solution.py:69
  9.2 0.9 copy-start.23
  9.2 1.2 copy-start.24
  9.2 59.1 %all-reduce.6.cloned.1.call-start = ((), (), s32[]{:S(2)}) async-start(), calls=%async_computation.6 | async-start | bytes 131072 | tf_op jit(solution)/shard_map/psum | solution.py:72
  29.6 2.4 copy-start.1
  33.8 213.5 %all-gather.8.cloned.1.call-start = ((), (), s32[]{:S(2)}) async-start(), calls=%async_computation.5 | async-start | bytes 1310720 | tf_op jit(solution)/shard_map/all_gather | solution.py:83
  34.6 8.4 %copy-start = (f32[128,2,4,256]{3,2,1,0:T(4,128)S(1)}, f32[128,2,4,256]{3,2,1,0:T(4,128)}, u32[]{:S(2)}) copy-start(f32[128,2,4,256]{3,2,1,0:T(4,128)} %param.15) | copy-start | bytes 3145732
  34.6 215.3 %all-gather.6.cloned.1.call-start = ((), (), s32[]{:S(2)}) async-start(), calls=%async_computation.4 | async-start | bytes 1310720 | tf_op jit(solution)/shard_map/all_gather | solution.py:82
  100.6 1.0 copy-start.12
  100.6 1.0 copy-start.26
  116.7 3.4 copy-start.5
  120.1 1.0 copy-start.43
  150.1 1.3 copy-start.4
  151.4 0.9 copy-start.18
  188.8 1.0 copy-start.14
  188.8 1.0 copy-start.27
  204.9 3.2 copy-start.6
  237.6 1.3 copy-start.3
  238.9 1.0 copy-start.19
  240.2 0.8 copy-start.15
  240.2 0.9 copy-start.17
  240.4 1.2 copy-start.9
  243.8 0.9 copy-start.10
  244.8 0.9 copy-start.8
  244.8 1.0 copy-start.20
  256.0 13.8 %all-to-all-start = ((f32[2,256,128]{2,0,1:T(2,128)}), f32[2,256,128]{2,0,1:T(2,128)}, u32[]{:S(2)}, u32[]{:S(2)}) async-start(f32[2,256,128]{2,0,1:T(2,128)} %copy.164), calls=%async_computation | async-start | bytes 524288 | tf_op jit(solution)/shard_map/all_to_all | solution.py:106
  262.7 1.7 copy-start.25
  273.4 3.3 copy-start.28
  273.4 3.3 copy-start.30
  281.3 29.7 %all-to-all-start.1 = ((f32[4,1,16384]{2,1,0:T(1,128)}), f32[4,1,16384]{2,1,0:T(1,128)}, u32[]{:S(2)}, u32[]{:S(2)}) async-start(f32[4,1,16384]{2,1,0:T(1,128)} %reshape.679), calls=%async_computation.1 | async-start | bytes 524288 | tf_op jit(solution)/shard_map/all_to_all | solution.py:114
  314.6 1.0 copy-start.2
  327.8 10.4 %all-to-all-start.2 = ((f32[2,256,128]{2,0,1:T(2,128)}), f32[2,256,128]{2,0,1:T(2,128)S(1)}, u32[]{:S(2)}, u32[]{:S(2)}) async-start(f32[2,256,128]{2,0,1:T(2,128)} %copy.180), calls=%async_computation.2 | async-start | bytes 524288 | tf_op jit(solution)/shard_map/all_to_all | solution.py:106
  (22 other events, 15.1 us)
Sparse Core Ops, SparseCore 0:
  10.1 19.4 all-gather.3
  33.9 34.3 all-reduce.5
  70.4 16.4 all-gather.7
  88.4 16.8 all-gather.5
where the time goes:
time: 374 us; the launch traced here: 367 us
  other arithmetic  141 us (38%)
  blocking collectives  59.1 us (16%)
  local copies, waits for them, and re-layouts  53.9 us (14%)
  waiting for transfers between devices  50.1 us (13%)
  matrix products  33 us (9%)
  between operations  17.2 us (5%)
  starting transfers between devices  11.7 us (3%)
    another operation x14, other arithmetic, invert(): lower_factor = jnp.linalg.cholesky(normal)  76.3 us
    another operation x5, other arithmetic, invert(): lax.linalg.triangular_solve(lower_factor, middle, left_side=True, lower=T...  44.8 us
    psum x2, blocking collectives, body(): coupling, own_energy = lax.psum((coupling, own_energy), 'pw')  39.1 us
    psum x1, waiting for transfers between devices, body(): forward_part, backward_part = lax.psum((forward_part, backward_part), 'pw')  20.5 us
    all_gather x1, waiting for transfers between devices, body(): every_wave = lax.all_gather(waves_flat, 'band', axis=0, tiled=True)  19 us
    unnamed x93, local copies, waits for them, and re-layouts  18.7 us
    another operation x15, local copies, waits for them, and re-layouts, invert(): lax.linalg.triangular_solve(lower_factor, middle, left_side=True, lower=T...  12.4 us
    all_to_all x2, waiting for transfers between devices, body(): lax.all_to_all(sectioned, 'pw', split_axis=1, concat_axis=2, tiled=True)  10.5 us
  transfers between devices with their start and end apart: 7, of which 4 were waited for; matrix products, arithmetic and copies ran while one was open for 49% of the time, Pallas kernels for 0%

commit v1 on v0

--- a/solution.py
+++ b/solution.py
@@ -1,8 +1,12 @@
+import functools
 import math
 
 import jax
 import jax.numpy as jnp
+import numpy as np
 from jax import lax
+from jax.experimental import pallas as pl
+from jax.experimental.pallas import tpu as pltpu
 from jax.sharding import PartitionSpec as P
 
 ITERS = 2
@@ -138,6 +142,390 @@
     return (solution, derivative)
 
 
+MESH = pl.DeviceIdType.MESH
+TILE = 8
+
+
+def halves(x):
+    high = x.astype(jnp.bfloat16)
+    return high, (x - high.astype(jnp.float32)).astype(jnp.bfloat16)
+
+
+def mul(a, b, turned=False):
+    dims = (((1,), (1 if turned else 0,)), ((), ()))
+    return lax.dot_general(a, b, dims, preferred_element_type=jnp.float32)
+
+
+def mul3(a, b, turned=False):
+    return mul(a[0], b[0], turned) + (mul(a[0], b[1], turned) + mul(a[1], b[0], turned))
+
+
+def exact(a, b):
+    return jnp.dot(a, b, precision=precise, preferred_element_type=jnp.float32)
+
+
+def local_plan_fits(args, mesh):
+    waves, projectors = args[0], args[3]
+    peers, groups = mesh.shape["pw"], mesh.shape["band"]
+    bands, rows, width = waves.shape[0], waves.shape[2], waves.shape[3]
+    return (
+        groups == 4
+        and rows == groups
+        and bands == TILE * peers
+        and bands * groups == 128
+        and projectors.shape[0] == 128
+        and peers * rows == 16
+        and width % 128 == 0
+        and projectors.size * peers * 4 <= 8 << 20
+    )
+
+
+def local_kernel(
+    peers, groups, sets, proj, pot, strengths, shifts, right_hi, right_lo, left_hi, left_lo,
+    resp, deriv,
+    got, marg, parts, whole, inv, both, made, field, answer, far, phi, plo, levels,
+    s_send, s_recv, r_send, r_recv, g_send, g_recv, t_send, t_recv,
+    p1_send, p1_recv, p2_send, p2_recv, p3_send, p3_recv, v_send, v_recv,
+    x_send, x_recv, d_send, d_recv, o_send, o_recv,
+):
+    kgrp = lax.axis_index("kgrp")
+    p = lax.axis_index("pw")
+    b = lax.axis_index("band")
+    core = lax.rem(b, 2)
+    side = b // 2
+    total = peers * groups
+    mine = p * groups + b
+    slot = p * 2 + side
+    width = sets.shape[4]
+    slab = groups * sets.shape[3]
+    points = float(total * width)
+    barrier = pltpu.get_barrier_semaphore()
+
+    def flat(o):
+        q = lax.rem(mine + o, total)
+        return q // groups, lax.rem(q, groups)
+
+    for o in range(1, total):
+        q, c = flat(o)
+        pl.semaphore_signal(barrier, inc=1, device_id=(kgrp, q, c), device_id_type=MESH)
+    pl.semaphore_wait(barrier, total - 1)
+
+    started = []
+
+    def send(source, target, ssem, rsem, q, c):
+        copy = pltpu.make_async_remote_copy(
+            src_ref=source, dst_ref=target, send_sem=ssem, recv_sem=rsem,
+            device_id=(kgrp, q, c), device_id_type=MESH,
+        )
+        copy.start()
+        started.append(copy)
+        return copy
+
+    first = []
+    for a in range(3):
+        for o in range(1, groups):
+            c = lax.rem(b + o, groups)
+            k = a * groups + o
+            first.append(send(sets.at[a, c], got.at[a, b], s_send.at[k], s_recv.at[k], p, c))
+    pots, pass1 = [], []
+    for o in range(1, peers):
+        q = lax.rem(p + o, peers)
+        pots.append(send(pot, levels.at[p], v_send.at[o], v_recv.at[o], q, b))
+    for o in range(1, peers):
+        q = lax.rem(p + o, peers)
+        pass1.append(send(proj.at[b], far.at[mine], p1_send.at[o], p1_recv.at[o], q, b))
+    for a in range(3):
+        got[a, b] = sets[a, b]
+    levels[p] = pot[...]
+
+    def set_of(a):
+        return got[a, :, 0].reshape(slab, width), got[a, :, 1].reshape(slab, width)
+
+    for copy in first[:3]:
+        copy.wait_recv()
+    wr, wi = set_of(0)
+    lhs = halves(
+        jnp.concatenate(
+            [jnp.concatenate([wr, wi], 1), jnp.concatenate([-wi, wr], 1)], 0
+        )
+        * (1.0 / points)
+    )
+    for m in range(2):
+        for copy in first[3 * m + 3 : 3 * m + 6]:
+            copy.wait_recv()
+        fr, fi = set_of(m + 1)
+        part = mul3(lhs, halves(jnp.concatenate([fr, fi], 1)), True)
+        marg[m] = part.reshape(marg.shape[1:])
+    second = []
+    for o in range(1, total):
+        q, c = flat(o)
+        second.append(
+            send(marg.at[lax.rem(c, 2), q * 2 + c // 2], parts.at[mine], r_send.at[o], r_recv.at[o], q, c)
+        )
+    parts[mine] = marg[core, slot]
+    def own_rows(r, carry):
+        hi, lo = halves(proj[r])
+        phi[p * groups + r] = hi
+        plo[p * groups + r] = lo
+        return carry
+
+    lax.fori_loop(0, groups, own_rows, 0)
+    for copy in second:
+        copy.wait_recv()
+    summed = parts[0]
+    for k in range(1, total):
+        summed = summed + parts[k]
+    whole[slot] = summed
+    third = []
+    size = total // 2
+    for o in range(1, size):
+        s = lax.rem(slot + o, size)
+        third.append(
+            send(whole.at[slot], whole.at[slot], g_send.at[o], g_recv.at[o], s // 2, lax.rem(s, 2) * 2 + core)
+        )
+    for copy in pass1:
+        copy.wait_recv()
+    across = lax.rem(b + 2, groups)
+    pass2 = []
+    for o in range(1, peers):
+        row = lax.rem(p + o, peers) * groups + b
+        pass2.append(send(far.at[row], far.at[row], p2_send.at[o], p2_recv.at[o], p, across))
+    for copy in third:
+        copy.wait_recv()
+    stacked = whole[...].reshape(2 * slab, slab)
+    ar, ai = stacked[:slab], stacked[slab:]
+    turned = stacked.T
+    inv[0] = exact(turned, stacked)
+    inv[1] = exact(turned, jnp.concatenate([ai, -ar], 0))
+    lane = lax.broadcasted_iota(jnp.int32, (slab, slab), 1)
+    line = lax.broadcasted_iota(jnp.int32, (slab, slab), 0)
+    lane1 = lax.broadcasted_iota(jnp.int32, (1, slab), 1)
+    line1 = lax.broadcasted_iota(jnp.int32, (slab, 1), 0)
+
+    def eliminate(k, carry):
+        nr, ni = inv[0], inv[1]
+        rr, ri = inv[0, pl.ds(k, 1), :], inv[1, pl.ds(k, 1), :]
+        hit = lane == k
+        cr = jnp.sum(jnp.where(hit, nr, 0.0), 1, keepdims=True)
+        ci = jnp.sum(jnp.where(hit, ni, 0.0), 1, keepdims=True)
+        own = lane1 == k
+        scale = 1.0 / jnp.sum(jnp.where(own, rr, 0.0), 1, keepdims=True)
+        sr = jnp.where(own, 1.0, rr) * scale
+        si = jnp.where(own, 0.0, ri) * scale
+        cr = jnp.where(line1 == k, -1.0, cr)
+        ci = jnp.where(line1 == k, 0.0, ci)
+        gone = jnp.logical_or(hit, line == k)
+        inv[0] = jnp.where(gone, 0.0, nr) - (cr * sr - ci * si)
+        inv[1] = jnp.where(gone, 0.0, ni) - (cr * si + ci * sr)
+        return carry
+
+    lax.fori_loop(0, slab, eliminate, 0)
+    kr, ki = inv[0], inv[1]
+    mixed = exact(
+        jnp.concatenate([jnp.concatenate([ar, -ai], 1), jnp.concatenate([-ai, -ar], 1)], 0),
+        jnp.concatenate([kr, ki], 0),
+    )
+    sign = (1 - 2 * core).astype(jnp.float32) / (2.0 * string_step)
+    both[core] = mixed * sign
+    sibling = side * 2 + 1 - core
+    swap = send(both.at[core], both.at[core], t_send, t_recv, p, sibling)
+    for copy in pass2:
+        copy.wait_recv()
+    pass3 = []
+    for o in range(1, peers):
+        for j in range(2):
+            row = lax.rem(p + o, peers) * groups + (b if j == 0 else across)
+            k = 2 * o + j
+            pass3.append(send(far.at[row], far.at[row], p3_send.at[k], p3_recv.at[k], p, sibling))
+    fr, fi = set_of(1)
+    br, bi = set_of(2)
+    rhs = halves(jnp.concatenate([fr, fi, br, bi], 0))
+    swap.wait_recv()
+    f, g = both[0], both[1]
+    tfr, tfi, tbr, tbi = f[:slab], f[slab:], g[:slab], g[slab:]
+    table = halves(
+        jnp.concatenate(
+            [
+                jnp.concatenate([tfr, -tfi, tbr, -tbi], 1),
+                jnp.concatenate([tfi, tfr, tbi, tbr], 1),
+            ],
+            0,
+        )
+    )
+    made[...] = mul3(table, rhs).reshape(made.shape)
+    fields, outs = [], []
+    for o in range(1, total):
+        q, c = flat(o)
+        rows = pl.ds(pl.multiple_of((c * peers + q) * TILE, TILE), TILE)
+        fields.append(send(made.at[:, rows], field.at[:, mine], x_send.at[o], x_recv.at[o], q, c))
+    span = slab // groups
+    for o in range(1, groups):
+        c = lax.rem(b + o, groups)
+        rows = pl.ds(pl.multiple_of(c * span, TILE), span)
+        outs.append(send(made.at[:, rows], deriv.at[b], d_send.at[o], d_recv.at[o], p, c))
+    field[:, mine] = made[:, pl.ds(pl.multiple_of((b * peers + p) * TILE, TILE), TILE)]
+    deriv[b] = made[:, pl.ds(pl.multiple_of(b * span, TILE), span)]
+    for copy in pass3:
+        copy.wait_recv()
+
+    def far_rows(t, carry):
+        row = lax.rem(p * groups + groups + t, total)
+        hi, lo = halves(far[row])
+        phi[row] = hi
+        plo[row] = lo
+        return carry
+
+    lax.fori_loop(0, total - groups, far_rows, 0)
+    for copy in pots:
+        copy.wait_recv()
+    share = width // peers
+    level = jnp.concatenate([levels[k][:, :share] for k in range(peers)], 1)
+    level = jnp.broadcast_to(level[:, None, :], (total, TILE, width)).reshape(total * TILE, width)
+    iu = lax.broadcasted_iota(jnp.int32, (total, TILE, width), 0)
+    iw = lax.broadcasted_iota(jnp.int32, (total, TILE, width), 2)
+    fu = jnp.where(iu < total // 2, iu, iu - total).astype(jnp.float32) / total
+    fw = jnp.where(iw < width // 2, iw, iw - width).astype(jnp.float32) / width
+    shift = shifts[pl.ds(pl.multiple_of(p * TILE, TILE), TILE), :]
+    diagonal = kinetic_scale * (fu * fu + fw * fw) + shift[None]
+    diagonal = diagonal.reshape(total * TILE, width)
+    scale = strengths[...] * (1.0 / points)
+    for copy in fields:
+        copy.wait_recv()
+
+    def transform(xr, xi):
+        y = mul3(halves(jnp.concatenate([xr, xi], 1)), (right_hi[...], right_lo[...]))
+        y = jnp.concatenate([y[:, :width], y[:, width:]], 0)
+        z = mul3((left_hi[...], left_lo[...]), halves(y))
+        return z[: total * TILE], z[total * TILE :]
+
+    def operate(dr, di):
+        yr, yi = transform(dr, di)
+        zr, zi = transform(yr * level, -(yi * level))
+        accr = jnp.zeros((2 * TILE, slab), jnp.float32)
+        acci = jnp.zeros((2 * TILE, slab), jnp.float32)
+        for i in range(total):
+            at = slice(i * TILE, i * TILE + TILE)
+            hi, lo = halves(jnp.concatenate([dr[at], di[at]], 0))
+            accr = accr + mul3((hi, lo), (phi[i, 0], plo[i, 0]), True)
+            acci = acci + mul3((hi, lo), (phi[i, 1], plo[i, 1]), True)
+        coupling = jnp.concatenate(
+            [accr[:TILE] + acci[TILE:], accr[TILE:] - acci[:TILE]], 0
+        ) * scale
+        c2 = halves(coupling)
+        outr, outi = [], []
+        for i in range(total):
+            ur = mul3(c2, (phi[i, 0], plo[i, 0]))
+            ui = mul3(c2, (phi[i, 1], plo[i, 1]))
+            outr.append(ur[:TILE] - ui[TILE:])
+            outi.append(ui[:TILE] + ur[TILE:])
+        return (
+            diagonal * dr + zr + jnp.concatenate(outr, 0),
+            diagonal * di - zi + jnp.concatenate(outi, 0),
+        )
+
+    def summed_over(x):
+        x = x.reshape(total, TILE, width)
+        return jnp.sum(jnp.sum(x, 0), 1, keepdims=True)
+
+    def spread(x):
+        return jnp.broadcast_to(x[None], (total, TILE, width)).reshape(total * TILE, width)
+
+    rr = -field[0].reshape(total * TILE, width)
+    ri = -field[1].reshape(total * TILE, width)
+    dr, di = rr, ri
+    norm_now = summed_over(rr * rr + ri * ri)
+    solr, soli = jnp.zeros_like(dr), jnp.zeros_like(di)
+    for turn in range(ITERS):
+        imr, imi = operate(dr, di)
+        curvature = summed_over(dr * imr + di * imi)
+        alpha = spread(norm_now / curvature)
+        solr, soli = solr + alpha * dr, soli + alpha * di
+        if turn + 1 < ITERS:
+            rr, ri = rr - alpha * imr, ri - alpha * imi
+            norm_next = summed_over(rr * rr + ri * ri)
+            beta = spread(norm_next / norm_now)
+            dr, di = rr + beta * dr, ri + beta * di
+            norm_now = norm_next
+    answer[0] = solr.reshape(total, TILE, width)
+    answer[1] = soli.reshape(total, TILE, width)
+    here = pl.ds(pl.multiple_of(p * TILE, TILE), TILE)
+    for o in range(1, peers):
+        q = lax.rem(p + o, peers)
+        outs.append(
+            send(answer.at[:, pl.ds(q * groups, groups)], resp.at[:, :, here], o_send.at[o], o_recv.at[o], q, b)
+        )
+    resp[:, :, here] = answer[:, pl.ds(p * groups, groups)]
+    for copy in outs:
+        copy.wait_recv()
+    for copy in started:
+        copy.wait_send()
+
+
+def tables(length, repeat):
+    index = np.arange(length)
+    angle = (index[:, None] * index[None, :] % length) * (2.0 * math.pi / length)
+    eye = np.eye(repeat)
+    cosine = np.kron(np.cos(angle) / math.sqrt(length), eye)
+    sine = np.kron(np.sin(angle) / math.sqrt(length), eye)
+    return cosine.astype(np.float32), sine.astype(np.float32)
+
+
+def split_table(table):
+    return halves(jnp.asarray(table))
+
+
+def local_body(mesh, waves, forward, backward, projectors, potential, strengths, shifts):
+    peers, groups = mesh.shape["pw"], mesh.shape["band"]
+    bands, _, rows, width = waves.shape
+    slab, total = bands * groups, peers * rows
+    sets = jnp.stack([waves, forward, backward]).transpose(0, 3, 2, 1, 4)
+    proj = projectors.transpose(2, 1, 0, 3)
+    pot = jnp.pad(potential.T, ((0, 0), (0, 128 - potential.shape[0] % 128)))
+    c, s = tables(width, 1)
+    right = split_table(np.block([[c, s], [-s, c]]))
+    c, s = tables(total, TILE)
+    left = split_table(np.block([[c, -s], [s, c]]))
+    f32 = jnp.float32
+    dma = pltpu.SemaphoreType.DMA
+    vmem = pl.BlockSpec(memory_space=pltpu.VMEM)
+    sems = []
+    for count in (3 * groups, total, total // 2):
+        sems += [dma((count,)), dma((count,))]
+    sems += [dma, dma]
+    for count in (peers, peers, 2 * peers, peers, total, groups, peers):
+        sems += [dma((count,)), dma((count,))]
+    resp, deriv = pl.pallas_call(
+        functools.partial(local_kernel, peers, groups),
+        out_shape=(
+            jax.ShapeDtypeStruct((2, rows, bands, width), f32),
+            jax.ShapeDtypeStruct((rows, 2, bands, width), f32),
+        ),
+        in_specs=[vmem] * 9,
+        out_specs=(vmem, vmem),
+        scratch_shapes=[
+            pltpu.VMEM((3, groups, 2, bands, width), f32),
+            pltpu.VMEM((2, total // 2, 4 * slab // total, slab), f32),
+            pltpu.VMEM((total, 4 * slab // total, slab), f32),
+            pltpu.VMEM((total // 2, 4 * slab // total, slab), f32),
+            pltpu.VMEM((2, slab, slab), f32),
+            pltpu.VMEM((2, 2 * slab, slab), f32),
+            pltpu.VMEM((2, slab, width), f32),
+            pltpu.VMEM((2, total, TILE, width), f32),
+            pltpu.VMEM((2, total, TILE, width), f32),
+            pltpu.VMEM((total, 2, slab, width), f32),
+            pltpu.VMEM((total, 2, slab, width), jnp.bfloat16),
+            pltpu.VMEM((total, 2, slab, width), jnp.bfloat16),
+            pltpu.VMEM((peers, total, pot.shape[1]), f32),
+        ]
+        + sems,
+        compiler_params=pltpu.CompilerParams(collective_id=0, has_side_effects=True, vmem_limit_bytes=48 << 20),
+    )(
+        sets, proj, pot, strengths.reshape(1, -1), shifts.reshape(-1, 1),
+        right[0], right[1], left[0], left[1],
+    )
+    return resp.transpose(2, 0, 1, 3), deriv.transpose(2, 1, 0, 3)
+
+
 def solution(mesh):
     in_specs = (
         P("band", "kgrp", "pw", None),
@@ -149,4 +537,9 @@
         P("band"),
     )
     out_specs = (P("band", "kgrp", "pw", None), P("band", "kgrp", "pw", None))
-    return jax.shard_map(body, mesh=mesh, in_specs=in_specs, out_specs=out_specs, check_vma=False)
+    def pick(*args):
+        if local_plan_fits(args, mesh):
+            return local_body(mesh, *args)
+        return body(*args)
+
+    return jax.shard_map(pick, mesh=mesh, in_specs=in_specs, out_specs=out_specs, check_vma=False)

time: 374 us -> 89.3 us (0.24); the launches traced: 367 us -> 89.1 us
  other arithmetic: 141 us -> 0.07 us
  Pallas kernels: 0 us -> 82.1 us
  blocking collectives: 59.1 us -> 0 us
  waiting for transfers between devices: 50.1 us -> 0 us
  local copies, waits for them, and re-layouts: 53.9 us -> 6.19 us
  matrix products: 33 us -> 0 us
  between operations: 17.2 us -> 0.71 us
  starting transfers between devices: 11.7 us -> 0 us
    another operation x26 -> x0, other arithmetic: 125 us -> none  [the longest x14 76.3 us: invert(): lower_factor = jnp.linalg.cholesky(normal)]
    pallas_call x0 -> x1, Pallas kernels: none -> 82.1 us  [local_body(): pl.pallas_call(functools.partial(local_kernel, peers, groups), out_shape=...]
    psum x3 -> x0, blocking collectives: 47.5 us -> none  [the longest x2 39.1 us: body(): coupling, own_energy = lax.psum((coupling, own_energy), 'pw')]
    dot_general x15 -> x0, matrix products: 24.7 us -> none  [the longest x3 7.25 us: combine(): return jnp.einsum('ixg,xyij->jyg', vectors, table, precision=precise)]
    psum x1 -> x0, waiting for transfers between devices: 20.5 us -> none  [body(): forward_part, backward_part = lax.psum((forward_part, backward_part), 'pw')]
    all_gather x3 -> x0, waiting for transfers between devices: 19 us -> none  [the longest x1 19 us: body(): every_wave = lax.all_gather(waves_flat, 'band', axis=0, tiled=True)]
    another operation x27 -> x1, local copies, waits for them, and re-layouts: 16.9 us -> 0.16 us  [local_body(): sets = jnp.stack([waves, forward, backward]).transpose(0, 3, 2, 1, 4)]
    unnamed x93 -> x22, local copies, waits for them, and re-layouts: 18.7 us -> 5.24 us
  transfers between devices with their start and end apart: 7 -> 0, of which waited for: 4 -> 0; matrix products, arithmetic and copies ran while one was open for 49% -> 0% of each run, Pallas kernels for 0% -> 0%
where the time goes in v1:
time: 89.3 us; the launch traced here: 89.1 us
  Pallas kernels  82.1 us (92%)
  local copies, waits for them, and re-layouts  6.19 us (7%)
    pallas_call x1, Pallas kernels, local_body(): pl.pallas_call(functools.partial(local_kernel, peers, groups), out_shape=...  82.1 us
    unnamed x22, local copies, waits for them, and re-layouts  5.24 us

profile of v1, /device:TPU:0, one launch (start us, length us, event | category | flops | bytes accessed | tf_op | source)
XLA Modules:
  0.0 89.1 jit_solution(8934946101958659568)
XLA Ops:
  0.6 0.0 copy-start.8
  0.6 0.7 pad.4.pot
  1.3 0.0 copy-done.8
  1.3 0.1 copy.15.shifts
  1.4 0.0 copy-start.6
  1.4 0.0 copy-start.7
  1.4 1.1 %copy.23 = f32[32,2,4,256]{3,0,1,2:T(8,128)S(1)} copy(f32[32,2,4,256]{3,2,1,0:T(4,128)} %param.9) | data formatting | bytes 524288 | tf_op args[0]
  2.5 0.0 copy-done.6
  2.5 0.0 copy-done.7
  2.6 0.2 copy_bitcast_fusion.1
  2.7 0.0 copy-start.5
  2.7 0.1 maximum_bitcast_fusion.sets
  2.8 1.1 %copy-done.5 = f32[128,2,4,256]{3,2,1,0:T(4,128)S(1)} copy-done((f32[128,2,4,256]{3,2,1,0:T(4,128)S(1)}, f32[128,2,4,256]{3,2,1,0:T(4,128)}, u32[]{:S(2)}) %copy-start.5) | copy-done | bytes 1048600
  4.0 0.0 copy-start
  4.0 0.0 copy-start.1
  4.0 0.0 copy-start.2
  4.0 0.0 copy-start.3
  4.0 0.3 copy.22
  4.3 0.0 copy-start.4
  4.3 0.7 copy-done
  5.0 0.2 copy-done.1
  5.2 0.0 copy-done.2
  5.2 0.0 copy-done.3
  5.2 0.0 copy-done.4
  5.2 82.1 %shard_map.104 = (f32[2,4,32,256]{3,2,1,0:T(8,128)S(1)}, f32[4,2,32,256]{3,2,1,0:T(8,128)S(1)}) custom-call(f32[3,4,2,32,256]{4,3,2,1,0:T(8,128)S(1)} %maximum_bitcast_fusion.sets, f32[4,2,128,256]{3,2,1,0:T(8,128)S(1)} %bitcast.17, f32[16,128]{1,0:T(8,128)S(1)} %pad.4.pot, f32[1,128]{1,0:T(1,128)S(1)} %bitcast.20, f32[32,1]{1,0:T(8,128)S(1)} %copy.15.shifts, ...), custom_call_target="tpu_custom_call" | custom-call | tf_op jit(solution)/shard_map/pallas_call | solution.py:497
  87.3 0.9 copy.16
  88.2 0.9 copy.17
Async XLA Ops:
  0.6 0.7 copy-start.8
  1.4 1.1 %copy-start.6 = (f32[32,2,4,256]{3,2,1,0:T(4,128)S(1)}, f32[32,2,4,256]{3,2,1,0:T(4,128)}, u32[]{:S(2)}) copy-start(f32[32,2,4,256]{3,2,1,0:T(4,128)} %param.11) | copy-start | bytes 786436
  1.4 1.1 %copy-start.7 = (f32[32,2,4,256]{3,2,1,0:T(4,128)S(1)}, f32[32,2,4,256]{3,2,1,0:T(4,128)}, u32[]{:S(2)}) copy-start(f32[32,2,4,256]{3,2,1,0:T(4,128)} %param.10) | copy-start | bytes 786436
  2.7 1.2 %copy-start.5 = (f32[128,2,4,256]{3,2,1,0:T(4,128)S(1)}, f32[128,2,4,256]{3,2,1,0:T(4,128)}, u32[]{:S(2)}) copy-start(f32[128,2,4,256]{3,2,1,0:T(4,128)} %param.12) | copy-start | bytes 3145732
  4.0 1.0 %copy-start = (bf16[512,512]{1,0:T(8,128)(2,1)S(1)}, bf16[512,512]{1,0:T(8,128)(2,1)}, u32[]{:S(2)}) copy-start(bf16[512,512]{1,0:T(8,128)(2,1)} %constant.14.right_lo) | copy-start | bytes 1572868
  4.0 1.2 %copy-start.1 = (bf16[512,512]{1,0:T(8,128)(2,1)S(1)}, bf16[512,512]{1,0:T(8,128)(2,1)}, u32[]{:S(2)}) copy-start(bf16[512,512]{1,0:T(8,128)(2,1)} %constant.11.right_hi) | copy-start | bytes 1572868
  4.0 1.2 %copy-start.2 = (bf16[256,256]{1,0:T(8,128)(2,1)S(1)}, bf16[256,256]{1,0:T(8,128)(2,1)}, u32[]{:S(2)}) copy-start(bf16[256,256]{1,0:T(8,128)(2,1)} %constant.18.left_lo) | copy-start | bytes 393220
  4.0 1.3 %copy-start.3 = (bf16[256,256]{1,0:T(8,128)(2,1)S(1)}, bf16[256,256]{1,0:T(8,128)(2,1)}, u32[]{:S(2)}) copy-start(bf16[256,256]{1,0:T(8,128)(2,1)} %constant.15.left_hi) | copy-start | bytes 393220
  4.3 0.9 %copy-start.4 = (f32[128]{0:T(128)S(1)}, f32[128]{0:T(128)}, u32[]{:S(2)}) copy-start(f32[128]{0:T(128)} %param.14) | copy-start | bytes 1540

commit v2 on v1

--- a/solution.py
+++ b/solution.py
@@ -227,13 +227,32 @@
             c = lax.rem(b + o, groups)
             k = a * groups + o
             first.append(send(sets.at[a, c], got.at[a, b], s_send.at[k], s_recv.at[k], p, c))
-    pots, pass1 = [], []
+    pots, pass1, pass2, pass3 = [], [], [], []
+    across = lax.rem(b + 2, groups)
+    sibling = side * 2 + 1 - core
     for o in range(1, peers):
         q = lax.rem(p + o, peers)
         pots.append(send(pot, levels.at[p], v_send.at[o], v_recv.at[o], q, b))
-    for o in range(1, peers):
-        q = lax.rem(p + o, peers)
-        pass1.append(send(proj.at[b], far.at[mine], p1_send.at[o], p1_recv.at[o], q, b))
+
+    def spread_half(half):
+        for o in range(1, peers):
+            q = lax.rem(p + o, peers)
+            k = half * peers + o
+            pass1.append(send(proj.at[b, half], far.at[mine, half], p1_send.at[k], p1_recv.at[k], q, b))
+
+    def cross_half(half):
+        for o in range(1, peers):
+            row = lax.rem(p + o, peers) * groups + b
+            k = half * peers + o
+            pass2.append(send(far.at[row, half], far.at[row, half], p2_send.at[k], p2_recv.at[k], p, across))
+
+    def share_rows(j):
+        for o in range(1, peers):
+            row = lax.rem(p + o, peers) * groups + (b if j == 0 else across)
+            k = 2 * o + j
+            pass3.append(send(far.at[row], far.at[row], p3_send.at[k], p3_recv.at[k], p, sibling))
+
+    spread_half(0)
     for a in range(3):
         got[a, b] = sets[a, b]
     levels[p] = pot[...]
@@ -283,13 +302,10 @@
         third.append(
             send(whole.at[slot], whole.at[slot], g_send.at[o], g_recv.at[o], s // 2, lax.rem(s, 2) * 2 + core)
         )
-    for copy in pass1:
-        copy.wait_recv()
-    across = lax.rem(b + 2, groups)
-    pass2 = []
-    for o in range(1, peers):
-        row = lax.rem(p + o, peers) * groups + b
-        pass2.append(send(far.at[row], far.at[row], p2_send.at[o], p2_recv.at[o], p, across))
+    for copy in pass1[: peers - 1]:
+        copy.wait_recv()
+    cross_half(0)
+    spread_half(1)
     for copy in third:
         copy.wait_recv()
     stacked = whole[...].reshape(2 * slab, slab)
@@ -319,7 +335,12 @@
         inv[1] = jnp.where(gone, 0.0, ni) - (cr * si + ci * sr)
         return carry
 
-    lax.fori_loop(0, slab, eliminate, 0)
+    lax.fori_loop(0, slab * 5 // 8, eliminate, 0)
+    for copy in pass1[peers - 1 :]:
+        copy.wait_recv()
+    cross_half(1)
+    share_rows(0)
+    lax.fori_loop(slab * 5 // 8, slab, eliminate, 0)
     kr, ki = inv[0], inv[1]
     mixed = exact(
         jnp.concatenate([jnp.concatenate([ar, -ai], 1), jnp.concatenate([-ai, -ar], 1)], 0),
@@ -327,16 +348,10 @@
     )
     sign = (1 - 2 * core).astype(jnp.float32) / (2.0 * string_step)
     both[core] = mixed * sign
-    sibling = side * 2 + 1 - core
     swap = send(both.at[core], both.at[core], t_send, t_recv, p, sibling)
     for copy in pass2:
         copy.wait_recv()
-    pass3 = []
-    for o in range(1, peers):
-        for j in range(2):
-            row = lax.rem(p + o, peers) * groups + (b if j == 0 else across)
-            k = 2 * o + j
-            pass3.append(send(far.at[row], far.at[row], p3_send.at[k], p3_recv.at[k], p, sibling))
+    share_rows(1)
     fr, fi = set_of(1)
     br, bi = set_of(2)
     rhs = halves(jnp.concatenate([fr, fi, br, bi], 0))
@@ -388,7 +403,6 @@
     shift = shifts[pl.ds(pl.multiple_of(p * TILE, TILE), TILE), :]
     diagonal = kinetic_scale * (fu * fu + fw * fw) + shift[None]
     diagonal = diagonal.reshape(total * TILE, width)
-    scale = strengths[...] * (1.0 / points)
     for copy in fields:
         copy.wait_recv()
 
@@ -398,9 +412,14 @@
         z = mul3((left_hi[...], left_lo[...]), halves(y))
         return z[: total * TILE], z[total * TILE :]
 
-    def operate(dr, di):
+    def energy(dr, di):
         yr, yi = transform(dr, di)
-        zr, zi = transform(yr * level, -(yi * level))
+        coupling = project(dr, di)
+        local = summed_over(diagonal * (dr * dr + di * di) + level * (yr * yr + yi * yi))
+        weight = jnp.sum(coupling * coupling * strengths[...], 1, keepdims=True) * points
+        return local + weight[:TILE] + weight[TILE:]
+
+    def project(dr, di):
         accr = jnp.zeros((2 * TILE, slab), jnp.float32)
         acci = jnp.zeros((2 * TILE, slab), jnp.float32)
         for i in range(total):
@@ -408,10 +427,14 @@
             hi, lo = halves(jnp.concatenate([dr[at], di[at]], 0))
             accr = accr + mul3((hi, lo), (phi[i, 0], plo[i, 0]), True)
             acci = acci + mul3((hi, lo), (phi[i, 1], plo[i, 1]), True)
-        coupling = jnp.concatenate(
+        return jnp.concatenate(
             [accr[:TILE] + acci[TILE:], accr[TILE:] - acci[:TILE]], 0
-        ) * scale
-        c2 = halves(coupling)
+        ) * (1.0 / points)
+
+    def operate(dr, di):
+        yr, yi = transform(dr, di)
+        zr, zi = transform(yr * level, -(yi * level))
+        c2 = halves(project(dr, di) * strengths[...])
         outr, outi = [], []
         for i in range(total):
             ur = mul3(c2, (phi[i, 0], plo[i, 0]))
@@ -436,8 +459,11 @@
     norm_now = summed_over(rr * rr + ri * ri)
     solr, soli = jnp.zeros_like(dr), jnp.zeros_like(di)
     for turn in range(ITERS):
-        imr, imi = operate(dr, di)
-        curvature = summed_over(dr * imr + di * imi)
+        if turn + 1 < ITERS:
+            imr, imi = operate(dr, di)
+            curvature = summed_over(dr * imr + di * imi)
+        else:
+            curvature = energy(dr, di)
         alpha = spread(norm_now / curvature)
         solr, soli = solr + alpha * dr, soli + alpha * di
         if turn + 1 < ITERS:
@@ -492,7 +518,7 @@
     for count in (3 * groups, total, total // 2):
         sems += [dma((count,)), dma((count,))]
     sems += [dma, dma]
-    for count in (peers, peers, 2 * peers, peers, total, groups, peers):
+    for count in (2 * peers, 2 * peers, 2 * peers, peers, total, groups, peers):
         sems += [dma((count,)), dma((count,))]
     resp, deriv = pl.pallas_call(
         functools.partial(local_kernel, peers, groups),

time: 89.3 us -> 81.4 us (0.912)
  Pallas kernels: 82.1 us -> 74.2 us
    pallas_call x1, Pallas kernels: 82.1 us -> 74.2 us  [local_body(): pl.pallas_call(functools.partial(local_kernel, peers, groups), out_shape=...]
where the time goes in v2:
time: 81.4 us; the launch traced here: 81.1 us
  Pallas kernels  74.2 us (91%)
  local copies, waits for them, and re-layouts  6.19 us (8%)
    pallas_call x1, Pallas kernels, local_body(): pl.pallas_call(functools.partial(local_kernel, peers, groups), out_shape=...  74.2 us
    unnamed x22, local copies, waits for them, and re-layouts  5.24 us

profile of v2, /device:TPU:0, one launch (start us, length us, event | category | flops | bytes accessed | tf_op | source)
XLA Modules:
  0.0 81.1 jit_solution(1875734633433309573)
XLA Ops:
  0.6 0.0 copy-start.8
  0.6 0.7 pad.4.pot
  1.3 0.0 copy-done.8
  1.3 0.1 copy.15.shifts
  1.4 0.0 copy-start.6
  1.4 0.0 copy-start.7
  1.4 1.1 %copy.23 = f32[32,2,4,256]{3,0,1,2:T(8,128)S(1)} copy(f32[32,2,4,256]{3,2,1,0:T(4,128)} %param.9) | data formatting | bytes 524288 | tf_op args[0]
  2.5 0.0 copy-done.6
  2.5 0.0 copy-done.7
  2.6 0.2 copy_bitcast_fusion.1
  2.7 0.0 copy-start.5
  2.7 0.1 maximum_bitcast_fusion.sets
  2.8 1.1 %copy-done.5 = f32[128,2,4,256]{3,2,1,0:T(4,128)S(1)} copy-done((f32[128,2,4,256]{3,2,1,0:T(4,128)S(1)}, f32[128,2,4,256]{3,2,1,0:T(4,128)}, u32[]{:S(2)}) %copy-start.5) | copy-done | bytes 1048600
  4.0 0.0 copy-start
  4.0 0.0 copy-start.1
  4.0 0.0 copy-start.2
  4.0 0.0 copy-start.3
  4.0 0.3 copy.22
  4.3 0.0 copy-start.4
  4.3 0.7 copy-done
  5.0 0.2 copy-done.1
  5.2 0.0 copy-done.2
  5.2 0.0 copy-done.3
  5.2 0.0 copy-done.4
  5.2 74.2 %shard_map.104 = (f32[2,4,32,256]{3,2,1,0:T(8,128)S(1)}, f32[4,2,32,256]{3,2,1,0:T(8,128)S(1)}) custom-call(f32[3,4,2,32,256]{4,3,2,1,0:T(8,128)S(1)} %maximum_bitcast_fusion.sets, f32[4,2,128,256]{3,2,1,0:T(8,128)S(1)} %bitcast.17, f32[16,128]{1,0:T(8,128)S(1)} %pad.4.pot, f32[1,128]{1,0:T(1,128)S(1)} %bitcast.20, f32[32,1]{1,0:T(8,128)S(1)} %copy.15.shifts, ...), custom_call_target="tpu_custom_call" | custom-call | tf_op jit(solution)/shard_map/pallas_call | solution.py:523
  79.4 0.9 %copy.16 = f32[32,2,4,256]{3,2,1,0:T(4,128)} copy(f32[32,2,4,256]{3,0,2,1:T(8,128)S(1)} %bitcast.19) | data formatting | bytes 524288
  80.3 0.9 %copy.17 = f32[32,2,4,256]{3,2,1,0:T(4,128)} copy(f32[32,2,4,256]{3,0,1,2:T(8,128)S(1)} %bitcast.18) | data formatting | bytes 524288
Async XLA Ops:
  0.6 0.7 copy-start.8
  1.4 1.1 %copy-start.6 = (f32[32,2,4,256]{3,2,1,0:T(4,128)S(1)}, f32[32,2,4,256]{3,2,1,0:T(4,128)}, u32[]{:S(2)}) copy-start(f32[32,2,4,256]{3,2,1,0:T(4,128)} %param.11) | copy-start | bytes 786436
  1.4 1.1 %copy-start.7 = (f32[32,2,4,256]{3,2,1,0:T(4,128)S(1)}, f32[32,2,4,256]{3,2,1,0:T(4,128)}, u32[]{:S(2)}) copy-start(f32[32,2,4,256]{3,2,1,0:T(4,128)} %param.10) | copy-start | bytes 786436
  2.7 1.2 %copy-start.5 = (f32[128,2,4,256]{3,2,1,0:T(4,128)S(1)}, f32[128,2,4,256]{3,2,1,0:T(4,128)}, u32[]{:S(2)}) copy-start(f32[128,2,4,256]{3,2,1,0:T(4,128)} %param.12) | copy-start | bytes 3145732
  4.0 1.0 %copy-start = (bf16[512,512]{1,0:T(8,128)(2,1)S(1)}, bf16[512,512]{1,0:T(8,128)(2,1)}, u32[]{:S(2)}) copy-start(bf16[512,512]{1,0:T(8,128)(2,1)} %constant.14.right_lo) | copy-start | bytes 1572868
  4.0 1.2 %copy-start.1 = (bf16[512,512]{1,0:T(8,128)(2,1)S(1)}, bf16[512,512]{1,0:T(8,128)(2,1)}, u32[]{:S(2)}) copy-start(bf16[512,512]{1,0:T(8,128)(2,1)} %constant.11.right_hi) | copy-start | bytes 1572868
  4.0 1.2 %copy-start.2 = (bf16[256,256]{1,0:T(8,128)(2,1)S(1)}, bf16[256,256]{1,0:T(8,128)(2,1)}, u32[]{:S(2)}) copy-start(bf16[256,256]{1,0:T(8,128)(2,1)} %constant.18.left_lo) | copy-start | bytes 393220
  4.0 1.3 %copy-start.3 = (bf16[256,256]{1,0:T(8,128)(2,1)S(1)}, bf16[256,256]{1,0:T(8,128)(2,1)}, u32[]{:S(2)}) copy-start(bf16[256,256]{1,0:T(8,128)(2,1)} %constant.15.left_hi) | copy-start | bytes 393220
  4.3 0.9 %copy-start.4 = (f32[128]{0:T(128)S(1)}, f32[128]{0:T(128)}, u32[]{:S(2)}) copy-start(f32[128]{0:T(128)} %param.14) | copy-start | bytes 1540

commit v3 on v2

--- a/solution.py
+++ b/solution.py
@@ -181,13 +181,14 @@
 
 
 def local_kernel(
-    peers, groups, sets, proj, pot, strengths, shifts, right_hi, right_lo, left_hi, left_lo,
+    peers, groups, waves, ahead, behind, proj, pot, strengths, shifts, right_hi, right_lo, left_hi, left_lo,
     resp, deriv,
-    got, marg, parts, whole, inv, both, made, field, answer, far, phi, plo, levels,
-    s_send, s_recv, r_send, r_recv, g_send, g_recv, t_send, t_recv,
+    got, marg, pair, merged, parts, whole, inv, both, made, field, answer, far, phi, plo, levels,
+    s_send, s_recv, m_send, m_recv, r_send, r_recv, g_send, g_recv, t_send, t_recv,
     p1_send, p1_recv, p2_send, p2_recv, p3_send, p3_recv, v_send, v_recv,
     x_send, x_recv, d_send, d_recv, o_send, o_recv,
 ):
+    sets = (waves, ahead, behind)
     kgrp = lax.axis_index("kgrp")
     p = lax.axis_index("pw")
     b = lax.axis_index("band")
@@ -196,8 +197,8 @@
     total = peers * groups
     mine = p * groups + b
     slot = p * 2 + side
-    width = sets.shape[4]
-    slab = groups * sets.shape[3]
+    width = waves.shape[3]
+    slab = groups * waves.shape[2]
     points = float(total * width)
     barrier = pltpu.get_barrier_semaphore()
 
@@ -226,7 +227,7 @@
         for o in range(1, groups):
             c = lax.rem(b + o, groups)
             k = a * groups + o
-            first.append(send(sets.at[a, c], got.at[a, b], s_send.at[k], s_recv.at[k], p, c))
+            first.append(send(sets[a].at[c], got.at[a, b], s_send.at[k], s_recv.at[k], p, c))
     pots, pass1, pass2, pass3 = [], [], [], []
     across = lax.rem(b + 2, groups)
     sibling = side * 2 + 1 - core
@@ -254,7 +255,7 @@
 
     spread_half(0)
     for a in range(3):
-        got[a, b] = sets[a, b]
+        got[a, b] = sets[a][b]
     levels[p] = pot[...]
 
     def set_of(a):
@@ -275,13 +276,18 @@
         fr, fi = set_of(m + 1)
         part = mul3(lhs, halves(jnp.concatenate([fr, fi], 1)), True)
         marg[m] = part.reshape(marg.shape[1:])
+    joined = send(marg.at[1 - core], pair, m_send, m_recv, p, sibling)
+    joined.wait_recv()
+    merged[...] = marg[core] + pair[...]
     second = []
-    for o in range(1, total):
-        q, c = flat(o)
+    size = total // 2
+    for o in range(1, size):
+        s = lax.rem(slot + o, size)
         second.append(
-            send(marg.at[lax.rem(c, 2), q * 2 + c // 2], parts.at[mine], r_send.at[o], r_recv.at[o], q, c)
-        )
-    parts[mine] = marg[core, slot]
+            send(merged.at[s], parts.at[slot], r_send.at[o], r_recv.at[o], s // 2, lax.rem(s, 2) * 2 + core)
+        )
+    parts[slot] = merged[slot]
+
     def own_rows(r, carry):
         hi, lo = halves(proj[r])
         phi[p * groups + r] = hi
@@ -292,11 +298,10 @@
     for copy in second:
         copy.wait_recv()
     summed = parts[0]
-    for k in range(1, total):
+    for k in range(1, size):
         summed = summed + parts[k]
     whole[slot] = summed
     third = []
-    size = total // 2
     for o in range(1, size):
         s = lax.rem(slot + o, size)
         third.append(
@@ -504,7 +509,7 @@
     peers, groups = mesh.shape["pw"], mesh.shape["band"]
     bands, _, rows, width = waves.shape
     slab, total = bands * groups, peers * rows
-    sets = jnp.stack([waves, forward, backward]).transpose(0, 3, 2, 1, 4)
+    sets = [x.transpose(2, 1, 0, 3) for x in (waves, forward, backward)]
     proj = projectors.transpose(2, 1, 0, 3)
     pot = jnp.pad(potential.T, ((0, 0), (0, 128 - potential.shape[0] % 128)))
     c, s = tables(width, 1)
@@ -515,9 +520,8 @@
     dma = pltpu.SemaphoreType.DMA
     vmem = pl.BlockSpec(memory_space=pltpu.VMEM)
     sems = []
-    for count in (3 * groups, total, total // 2):
-        sems += [dma((count,)), dma((count,))]
-    sems += [dma, dma]
+    for count in ((3 * groups,), (), (total // 2,), (total // 2,), ()):
+        sems += [dma(count) if count else dma, dma(count) if count else dma]
     for count in (2 * peers, 2 * peers, 2 * peers, peers, total, groups, peers):
         sems += [dma((count,)), dma((count,))]
     resp, deriv = pl.pallas_call(
@@ -526,12 +530,14 @@
             jax.ShapeDtypeStruct((2, rows, bands, width), f32),
             jax.ShapeDtypeStruct((rows, 2, bands, width), f32),
         ),
-        in_specs=[vmem] * 9,
+        in_specs=[vmem] * 11,
         out_specs=(vmem, vmem),
         scratch_shapes=[
             pltpu.VMEM((3, groups, 2, bands, width), f32),
             pltpu.VMEM((2, total // 2, 4 * slab // total, slab), f32),
-            pltpu.VMEM((total, 4 * slab // total, slab), f32),
+            pltpu.VMEM((total // 2, 4 * slab // total, slab), f32),
+            pltpu.VMEM((total // 2, 4 * slab // total, slab), f32),
+            pltpu.VMEM((total // 2, 4 * slab // total, slab), f32),
             pltpu.VMEM((total // 2, 4 * slab // total, slab), f32),
             pltpu.VMEM((2, slab, slab), f32),
             pltpu.VMEM((2, 2 * slab, slab), f32),
@@ -546,7 +552,7 @@
         + sems,
         compiler_params=pltpu.CompilerParams(collective_id=0, has_side_effects=True, vmem_limit_bytes=48 << 20),
     )(
-        sets, proj, pot, strengths.reshape(1, -1), shifts.reshape(-1, 1),
+        *sets, proj, pot, strengths.reshape(1, -1), shifts.reshape(-1, 1),
         right[0], right[1], left[0], left[1],
     )
     return resp.transpose(2, 0, 1, 3), deriv.transpose(2, 1, 0, 3)

time: 81.4 us -> 80.9 us (level)
  Pallas kernels: 74.2 us -> 73.3 us
    unnamed x22 -> x16, local copies, waits for them, and re-layouts: 5.24 us -> 4.01 us
    transpose x0 -> x1, local copies, waits for them, and re-layouts: none -> 1.19 us  [local_body(): sets = [x.transpose(2, 1, 0, 3) for x in (waves, forward, backward)]]
    pallas_call x1, Pallas kernels: 74.2 us -> 73.3 us  [local_body(): pl.pallas_call(functools.partial(local_kernel, peers, groups), out_shape=...]
where the time goes in v3:
time: 80.9 us; the launch traced here: 80.7 us
  Pallas kernels  73.3 us (91%)
  local copies, waits for them, and re-layouts  6.72 us (8%)
    pallas_call x1, Pallas kernels, local_body(): pl.pallas_call(functools.partial(local_kernel, peers, groups), out_shape=...  73.3 us
    unnamed x16, local copies, waits for them, and re-layouts  4.01 us

profile of v3, /device:TPU:0, one launch (start us, length us, event | category | flops | bytes accessed | tf_op | source)
XLA Modules:
  0.0 80.7 jit_solution(8865287888237455933)
XLA Ops:
  0.6 0.0 copy-start.5
  0.6 0.8 pad.4.pot
  1.4 0.7 copy.15.shifts
  2.2 1.0 %copy.23 = f32[32,2,4,256]{3,0,1,2:T(8,128)S(1)} copy(f32[32,2,4,256]{3,2,1,0:T(4,128)} %param.9) | data formatting | bytes 524288 | tf_op args[0]
  3.2 1.2 %copy_bitcast_fusion.1 = (f32[4,2,32,256]{3,2,1,0:T(8,128)S(1)}, f32[4,2,32,256]{3,2,1,0:T(8,128)S(1)}) fusion(f32[32,2,4,256]{3,2,1,0:T(4,128)} %param.11, f32[32,2,4,256]{3,2,1,0:T(4,128)} %param.10), kind=kLoop, calls=%fused_computation.1 | loop fusion | bytes 1048576 | tf_op jit(solution)/shard_map/transpose | solution.py:512
  4.4 0.0 copy-done.5
  4.4 0.0 copy-start
  4.4 0.0 copy-start.1
  4.4 0.0 copy-start.2
  4.4 0.0 copy-start.3
  4.5 0.3 copy.22
  4.8 0.0 copy-start.4
  4.8 0.6 copy-done
  5.5 0.2 copy-done.1
  5.6 0.0 copy-done.2
  5.6 0.0 copy-done.3
  5.7 0.0 copy-done.4
  5.7 73.3 %shard_map.104 = (f32[2,4,32,256]{3,2,1,0:T(8,128)S(1)}, f32[4,2,32,256]{3,2,1,0:T(8,128)S(1)}) custom-call(f32[4,2,32,256]{3,2,1,0:T(8,128)S(1)} %bitcast.16, f32[4,2,32,256]{3,2,1,0:T(8,128)S(1)} %get-tuple-element.9.ahead, f32[4,2,32,256]{3,2,1,0:T(8,128)S(1)} %get-tuple-element.8.behind, f32[4,2,128,256]{3,2,1,0:T(8,128)S(1)} %bitcast.15, ...), custom_call_target="tpu_custom_call" | custom-call | tf_op jit(solution)/shard_map/pallas_call | solution.py:527
  79.0 0.9 %copy.16 = f32[32,2,4,256]{3,2,1,0:T(4,128)} copy(f32[32,2,4,256]{3,0,2,1:T(8,128)S(1)} %bitcast.18) | data formatting | bytes 524288
  79.8 0.9 %copy.17 = f32[32,2,4,256]{3,2,1,0:T(4,128)} copy(f32[32,2,4,256]{3,0,1,2:T(8,128)S(1)} %bitcast.17) | data formatting | bytes 524288
Async XLA Ops:
  0.6 3.8 %copy-start.5 = (f32[128,2,4,256]{3,2,1,0:T(4,128)S(1)}, f32[128,2,4,256]{3,2,1,0:T(4,128)}, u32[]{:S(2)}) copy-start(f32[128,2,4,256]{3,2,1,0:T(4,128)} %param.12) | copy-start | bytes 3145732
  4.4 1.0 %copy-start = (bf16[512,512]{1,0:T(8,128)(2,1)S(1)}, bf16[512,512]{1,0:T(8,128)(2,1)}, u32[]{:S(2)}) copy-start(bf16[512,512]{1,0:T(8,128)(2,1)} %constant.14.right_lo) | copy-start | bytes 1572868
  4.4 1.2 %copy-start.1 = (bf16[512,512]{1,0:T(8,128)(2,1)S(1)}, bf16[512,512]{1,0:T(8,128)(2,1)}, u32[]{:S(2)}) copy-start(bf16[512,512]{1,0:T(8,128)(2,1)} %constant.11.right_hi) | copy-start | bytes 1572868
  4.4 1.2 %copy-start.2 = (bf16[256,256]{1,0:T(8,128)(2,1)S(1)}, bf16[256,256]{1,0:T(8,128)(2,1)}, u32[]{:S(2)}) copy-start(bf16[256,256]{1,0:T(8,128)(2,1)} %constant.18.left_lo) | copy-start | bytes 393220
  4.4 1.2 %copy-start.3 = (bf16[256,256]{1,0:T(8,128)(2,1)S(1)}, bf16[256,256]{1,0:T(8,128)(2,1)}, u32[]{:S(2)}) copy-start(bf16[256,256]{1,0:T(8,128)(2,1)} %constant.15.left_hi) | copy-start | bytes 393220
  4.8 0.9 %copy-start.4 = (f32[128]{0:T(128)S(1)}, f32[128]{0:T(128)}, u32[]{:S(2)}) copy-start(f32[128]{0:T(128)} %param.14) | copy-start | bytes 1540

commit v4 on v3

--- a/solution.py
+++ b/solution.py
@@ -235,17 +235,20 @@
         q = lax.rem(p + o, peers)
         pots.append(send(pot, levels.at[p], v_send.at[o], v_recv.at[o], q, b))
 
+    cut = slab * 11 // 16 // TILE * TILE
+    chunks = (pl.ds(0, cut), pl.ds(cut, slab - cut))
+
     def spread_half(half):
         for o in range(1, peers):
             q = lax.rem(p + o, peers)
             k = half * peers + o
-            pass1.append(send(proj.at[b, half], far.at[mine, half], p1_send.at[k], p1_recv.at[k], q, b))
+            pass1.append(send(proj.at[b, :, chunks[half]], far.at[mine, :, chunks[half]], p1_send.at[k], p1_recv.at[k], q, b))
 
     def cross_half(half):
         for o in range(1, peers):
             row = lax.rem(p + o, peers) * groups + b
             k = half * peers + o
-            pass2.append(send(far.at[row, half], far.at[row, half], p2_send.at[k], p2_recv.at[k], p, across))
+            pass2.append(send(far.at[row, :, chunks[half]], far.at[row, :, chunks[half]], p2_send.at[k], p2_recv.at[k], p, across))
 
     def share_rows(j):
         for o in range(1, peers):
@@ -340,12 +343,12 @@
         inv[1] = jnp.where(gone, 0.0, ni) - (cr * si + ci * sr)
         return carry
 
-    lax.fori_loop(0, slab * 5 // 8, eliminate, 0)
+    lax.fori_loop(0, slab // 2, eliminate, 0)
     for copy in pass1[peers - 1 :]:
         copy.wait_recv()
     cross_half(1)
     share_rows(0)
-    lax.fori_loop(slab * 5 // 8, slab, eliminate, 0)
+    lax.fori_loop(slab // 2, slab, eliminate, 0)
     kr, ki = inv[0], inv[1]
     mixed = exact(
         jnp.concatenate([jnp.concatenate([ar, -ai], 1), jnp.concatenate([-ai, -ar], 1)], 0),

time: 80.9 us -> 83 us (1.026)
  Pallas kernels: 73.3 us -> 75.4 us
    pallas_call x1, Pallas kernels: 73.3 us -> 75.4 us  [local_body(): pl.pallas_call(functools.partial(local_kernel, peers, groups), out_shape=...]
where the time goes in v4:
time: 83 us; the launch traced here: 82.8 us
  Pallas kernels  75.4 us (91%)
  local copies, waits for them, and re-layouts  6.72 us (8%)
    pallas_call x1, Pallas kernels, local_body(): pl.pallas_call(functools.partial(local_kernel, peers, groups), out_shape=...  75.4 us
    unnamed x16, local copies, waits for them, and re-layouts  4.01 us

profile of v4, /device:TPU:0, one launch (start us, length us, event | category | flops | bytes accessed | tf_op | source)
XLA Modules:
  0.0 82.8 jit_solution(9829240445167119377)
XLA Ops:
  0.6 0.0 copy-start.5
  0.6 0.8 pad.4.pot
  1.4 0.7 copy.15.shifts
  2.2 1.0 %copy.23 = f32[32,2,4,256]{3,0,1,2:T(8,128)S(1)} copy(f32[32,2,4,256]{3,2,1,0:T(4,128)} %param.9) | data formatting | bytes 524288 | tf_op args[0]
  3.2 1.2 %copy_bitcast_fusion.1 = (f32[4,2,32,256]{3,2,1,0:T(8,128)S(1)}, f32[4,2,32,256]{3,2,1,0:T(8,128)S(1)}) fusion(f32[32,2,4,256]{3,2,1,0:T(4,128)} %param.11, f32[32,2,4,256]{3,2,1,0:T(4,128)} %param.10), kind=kLoop, calls=%fused_computation.1 | loop fusion | bytes 1048576 | tf_op jit(solution)/shard_map/transpose | solution.py:515
  4.4 0.0 copy-done.5
  4.4 0.0 copy-start
  4.4 0.0 copy-start.1
  4.4 0.0 copy-start.2
  4.4 0.0 copy-start.3
  4.5 0.3 copy.22
  4.8 0.0 copy-start.4
  4.8 0.6 copy-done
  5.5 0.2 copy-done.1
  5.6 0.0 copy-done.2
  5.6 0.0 copy-done.3
  5.7 0.0 copy-done.4
  5.7 75.4 %shard_map.104 = (f32[2,4,32,256]{3,2,1,0:T(8,128)S(1)}, f32[4,2,32,256]{3,2,1,0:T(8,128)S(1)}) custom-call(f32[4,2,32,256]{3,2,1,0:T(8,128)S(1)} %bitcast.16, f32[4,2,32,256]{3,2,1,0:T(8,128)S(1)} %get-tuple-element.9.ahead, f32[4,2,32,256]{3,2,1,0:T(8,128)S(1)} %get-tuple-element.8.behind, f32[4,2,128,256]{3,2,1,0:T(8,128)S(1)} %bitcast.15, ...), custom_call_target="tpu_custom_call" | custom-call | tf_op jit(solution)/shard_map/pallas_call | solution.py:530
  81.0 0.9 %copy.16 = f32[32,2,4,256]{3,2,1,0:T(4,128)} copy(f32[32,2,4,256]{3,0,2,1:T(8,128)S(1)} %bitcast.18) | data formatting | bytes 524288
  81.9 0.9 %copy.17 = f32[32,2,4,256]{3,2,1,0:T(4,128)} copy(f32[32,2,4,256]{3,0,1,2:T(8,128)S(1)} %bitcast.17) | data formatting | bytes 524288
Async XLA Ops:
  0.6 3.8 %copy-start.5 = (f32[128,2,4,256]{3,2,1,0:T(4,128)S(1)}, f32[128,2,4,256]{3,2,1,0:T(4,128)}, u32[]{:S(2)}) copy-start(f32[128,2,4,256]{3,2,1,0:T(4,128)} %param.12) | copy-start | bytes 3145732
  4.4 1.0 %copy-start = (bf16[512,512]{1,0:T(8,128)(2,1)S(1)}, bf16[512,512]{1,0:T(8,128)(2,1)}, u32[]{:S(2)}) copy-start(bf16[512,512]{1,0:T(8,128)(2,1)} %constant.14.right_lo) | copy-start | bytes 1572868
  4.4 1.2 %copy-start.1 = (bf16[512,512]{1,0:T(8,128)(2,1)S(1)}, bf16[512,512]{1,0:T(8,128)(2,1)}, u32[]{:S(2)}) copy-start(bf16[512,512]{1,0:T(8,128)(2,1)} %constant.11.right_hi) | copy-start | bytes 1572868
  4.4 1.2 %copy-start.2 = (bf16[256,256]{1,0:T(8,128)(2,1)S(1)}, bf16[256,256]{1,0:T(8,128)(2,1)}, u32[]{:S(2)}) copy-start(bf16[256,256]{1,0:T(8,128)(2,1)} %constant.18.left_lo) | copy-start | bytes 393220
  4.4 1.2 %copy-start.3 = (bf16[256,256]{1,0:T(8,128)(2,1)S(1)}, bf16[256,256]{1,0:T(8,128)(2,1)}, u32[]{:S(2)}) copy-start(bf16[256,256]{1,0:T(8,128)(2,1)} %constant.15.left_hi) | copy-start | bytes 393220
  4.8 0.9 %copy-start.4 = (f32[128]{0:T(128)S(1)}, f32[128]{0:T(128)}, u32[]{:S(2)}) copy-start(f32[128]{0:T(128)} %param.14) | copy-start | bytes 1540

commit v5 on v4

--- a/solution.py
+++ b/solution.py
@@ -235,7 +235,7 @@
         q = lax.rem(p + o, peers)
         pots.append(send(pot, levels.at[p], v_send.at[o], v_recv.at[o], q, b))
 
-    cut = slab * 11 // 16 // TILE * TILE
+    cut = slab // 2 // TILE * TILE
     chunks = (pl.ds(0, cut), pl.ds(cut, slab - cut))
 
     def spread_half(half):
@@ -343,12 +343,12 @@
         inv[1] = jnp.where(gone, 0.0, ni) - (cr * si + ci * sr)
         return carry
 
-    lax.fori_loop(0, slab // 2, eliminate, 0)
+    lax.fori_loop(0, slab * 5 // 8, eliminate, 0, unroll=4)
     for copy in pass1[peers - 1 :]:
         copy.wait_recv()
     cross_half(1)
     share_rows(0)
-    lax.fori_loop(slab // 2, slab, eliminate, 0)
+    lax.fori_loop(slab * 5 // 8, slab, eliminate, 0, unroll=4)
     kr, ki = inv[0], inv[1]
     mixed = exact(
         jnp.concatenate([jnp.concatenate([ar, -ai], 1), jnp.concatenate([-ai, -ar], 1)], 0),
@@ -401,8 +401,7 @@
     lax.fori_loop(0, total - groups, far_rows, 0)
     for copy in pots:
         copy.wait_recv()
-    share = width // peers
-    level = jnp.concatenate([levels[k][:, :share] for k in range(peers)], 1)
+    level = jnp.concatenate([levels[k] for k in range(peers)], 1)
     level = jnp.broadcast_to(level[:, None, :], (total, TILE, width)).reshape(total * TILE, width)
     iu = lax.broadcasted_iota(jnp.int32, (total, TILE, width), 0)
     iw = lax.broadcasted_iota(jnp.int32, (total, TILE, width), 2)
@@ -514,7 +513,7 @@
     slab, total = bands * groups, peers * rows
     sets = [x.transpose(2, 1, 0, 3) for x in (waves, forward, backward)]
     proj = projectors.transpose(2, 1, 0, 3)
-    pot = jnp.pad(potential.T, ((0, 0), (0, 128 - potential.shape[0] % 128)))
+    pot = potential.T
     c, s = tables(width, 1)
     right = split_table(np.block([[c, s], [-s, c]]))
     c, s = tables(total, TILE)

time: 83 us -> 81.5 us (0.982)
  Pallas kernels: 75.4 us -> 74.5 us
    unnamed x16 -> x18, local copies, waits for them, and re-layouts: 4.01 us -> 4 us
where the time goes in v5:
time: 81.5 us; the launch traced here: 81.3 us
  Pallas kernels  74.5 us (91%)
  local copies, waits for them, and re-layouts  6.02 us (7%)
    pallas_call x1, Pallas kernels, local_body(): pl.pallas_call(functools.partial(local_kernel, peers, groups), out_shape=...  74.5 us
    unnamed x18, local copies, waits for them, and re-layouts  4 us

profile of v5, /device:TPU:0, one launch (start us, length us, event | category | flops | bytes accessed | tf_op | source)
XLA Modules:
  0.0 81.3 jit_solution(10222116202831113598)
XLA Ops:
  0.6 0.0 copy-start.6
  0.6 0.8 %copy.15.shifts = f32[32,1]{1,0:T(8,128)S(1)} copy(f32[32,1]{0,1:T(1,128)} %bitcast.21) | data formatting | bytes 256 | tf_op jit(solution)/shard_map/reshape | solution.py:557
  1.5 1.0 %copy.23 = f32[32,2,4,256]{3,0,1,2:T(8,128)S(1)} copy(f32[32,2,4,256]{3,2,1,0:T(4,128)} %param.9) | data formatting | bytes 524288 | tf_op args[0]
  2.5 1.2 %copy_bitcast_fusion.1 = (f32[4,2,32,256]{3,2,1,0:T(8,128)S(1)}, f32[4,2,32,256]{3,2,1,0:T(8,128)S(1)}) fusion(f32[32,2,4,256]{3,2,1,0:T(4,128)} %param.11, f32[32,2,4,256]{3,2,1,0:T(4,128)} %param.10), kind=kLoop, calls=%fused_computation.1 | loop fusion | bytes 1048576 | tf_op jit(solution)/shard_map/transpose | solution.py:514
  3.7 0.0 copy-done.6
  3.7 0.0 copy-start
  3.7 0.0 copy-start.1
  3.7 0.0 copy-start.2
  3.7 0.0 copy-start.3
  3.8 0.0 copy-start.4
  3.8 0.3 copy.22
  4.1 0.0 copy-start.5
  4.1 0.6 copy-done
  4.8 0.2 copy-done.1
  4.9 0.0 copy-done.2
  4.9 0.0 copy-done.3
  5.0 0.0 copy-done.4
  5.0 0.0 copy-done.5
  5.0 74.5 %shard_map.104 = (f32[2,4,32,256]{3,2,1,0:T(8,128)S(1)}, f32[4,2,32,256]{3,2,1,0:T(8,128)S(1)}) custom-call(f32[4,2,32,256]{3,2,1,0:T(8,128)S(1)} %bitcast.16, f32[4,2,32,256]{3,2,1,0:T(8,128)S(1)} %get-tuple-element.9.ahead, f32[4,2,32,256]{3,2,1,0:T(8,128)S(1)} %get-tuple-element.8.behind, f32[4,2,128,256]{3,2,1,0:T(8,128)S(1)} %bitcast.15, ...), custom_call_target="tpu_custom_call" | custom-call | tf_op jit(solution)/shard_map/pallas_call | solution.py:529
  79.5 0.9 %copy.16 = f32[32,2,4,256]{3,2,1,0:T(4,128)} copy(f32[32,2,4,256]{3,0,2,1:T(8,128)S(1)} %bitcast.18) | data formatting | bytes 524288
  80.4 0.9 %copy.17 = f32[32,2,4,256]{3,2,1,0:T(4,128)} copy(f32[32,2,4,256]{3,0,1,2:T(8,128)S(1)} %bitcast.17) | data formatting | bytes 524288
Async XLA Ops:
  0.6 3.1 %copy-start.6 = (f32[128,2,4,256]{3,2,1,0:T(4,128)S(1)}, f32[128,2,4,256]{3,2,1,0:T(4,128)}, u32[]{:S(2)}) copy-start(f32[128,2,4,256]{3,2,1,0:T(4,128)} %param.12) | copy-start | bytes 3145732
  3.7 1.0 %copy-start = (bf16[512,512]{1,0:T(8,128)(2,1)S(1)}, bf16[512,512]{1,0:T(8,128)(2,1)}, u32[]{:S(2)}) copy-start(bf16[512,512]{1,0:T(8,128)(2,1)} %constant.9.right_lo) | copy-start | bytes 1572868
  3.7 1.2 %copy-start.1 = (bf16[512,512]{1,0:T(8,128)(2,1)S(1)}, bf16[512,512]{1,0:T(8,128)(2,1)}, u32[]{:S(2)}) copy-start(bf16[512,512]{1,0:T(8,128)(2,1)} %constant.6.right_hi) | copy-start | bytes 1572868
  3.7 1.2 %copy-start.2 = (bf16[256,256]{1,0:T(8,128)(2,1)S(1)}, bf16[256,256]{1,0:T(8,128)(2,1)}, u32[]{:S(2)}) copy-start(bf16[256,256]{1,0:T(8,128)(2,1)} %constant.13.left_lo) | copy-start | bytes 393220
  3.7 1.2 %copy-start.3 = (bf16[256,256]{1,0:T(8,128)(2,1)S(1)}, bf16[256,256]{1,0:T(8,128)(2,1)}, u32[]{:S(2)}) copy-start(bf16[256,256]{1,0:T(8,128)(2,1)} %constant.10.left_hi) | copy-start | bytes 393220
  3.8 1.2 %copy-start.4 = (f32[64,16]{0,1:T(8,128)S(1)}, f32[64,16]{0,1:T(8,128)}, u32[]{:S(2)}) copy-start(f32[64,16]{0,1:T(8,128)} %param.13) | copy-start | bytes 12292
  4.1 0.9 %copy-start.5 = (f32[128]{0:T(128)S(1)}, f32[128]{0:T(128)}, u32[]{:S(2)}) copy-start(f32[128]{0:T(128)} %param.14) | copy-start | bytes 1540
